TPU v7x, 32 devices: a whole 2x2x4 slice. The times are simulated.
32 devices in a mesh: dp: 2 (over y), ep: 16 (over z, x, core).
Axes of the slice: x: 2, y: 2, z: 4, core: 2. Of those that a mesh axis runs over, the one named last changes fastest.
Arguments:
- tokens: bfloat16 [16, 2, 1, 3584], P('ep', 'dp'), may hold values from -6 to 6
- gate_weights: bfloat16 [16, 2, 1, 8], P('ep', 'dp'), may hold values from 0.099609375 to 0.59765625
- expert_ids: int32 [16, 2, 1, 8], P('ep', 'dp'), may hold values from 0 to 15, all different within a row; in each aligned block of 2 rows (0 to 1, 2 to 3, ..., all dimensions but the last counted through in order) at most 2 rows name the same one
- gate_proj: bfloat16 [16, 3584, 2048], P('ep', None, 'dp'), may hold values from -0.09375 to 0.09375
- up_proj: bfloat16 [16, 3584, 2048], P('ep', None, 'dp'), may hold values from -0.09375 to 0.09375
- down_proj: bfloat16 [16, 2048, 3584], P('ep', 'dp'), may hold values from -0.125 to 0.125
Outputs:
- mixed: bfloat16 [16, 2, 1, 3584], P('ep', 'dp')
Inputs may be any that keep to these rules, and one draw needn't show every extreme that they name: `expert_ids`: each token names 8 different experts. Among the 2 tokens of one index of the first dimension, no expert is named more than 2 times, a bound that some block reaches.
All inputs are finite; a program needn't handle non-finite values.
Results may differ from a plain program's by a relative error of at most 0.02.
Values may be sent and summed in bfloat16 or wider, within the bound.
A program may use at most 64 MiB of HBM per device.

v0:
```python
import jax
import jax.numpy as jnp
from jax import lax
from jax.sharding import PartitionSpec as P


def placing(flat_ids, expert_count, capacity):
    labels = jnp.arange(expert_count, dtype=jnp.int32)
    onehot = (flat_ids[:, None] == labels[None, :]).astype(jnp.int32)
    earlier = jnp.cumsum(onehot, axis=0) - onehot
    slot_index = jnp.sum(earlier * onehot, axis=1)
    destination = flat_ids * capacity + slot_index
    targets = jnp.arange(expert_count * capacity, dtype=jnp.int32)
    return (destination[:, None] == targets[None, :]).astype(jnp.float32)


def body(tokens, gate_weights, expert_ids, gate_proj, up_proj, down_proj):
    group_count = lax.axis_size("dp")
    expert_count = lax.axis_size("ep")
    token_count = tokens.shape[2]
    feature_count = tokens.shape[3]
    top_count = expert_ids.shape[3]
    capacity = min(
        group_count * token_count, token_count * (group_count * top_count // expert_count + 1)
    )
    token_total = group_count * token_count
    slot_total = expert_count * capacity
    column_count = feature_count // group_count
    all_ids = lax.all_gather(expert_ids, "dp", axis=1, tiled=True)
    placed = placing(all_ids.reshape(-1), expert_count, capacity)
    selection = jnp.sum(placed.reshape(token_total, top_count, slot_total), axis=1)
    selection_t = selection.T.astype(jnp.bfloat16)
    token_rows, all_weights = (
        lax.all_gather(tokens, "dp", axis=1, tiled=True),
        lax.all_gather(gate_weights, "dp", axis=1, tiled=True),
    )
    buffer = jnp.dot(
        selection_t,
        token_rows.reshape(token_total, feature_count),
        preferred_element_type=jnp.float32,
    ).astype(jnp.bfloat16)
    received = lax.all_to_all(
        buffer.reshape(expert_count, capacity, feature_count),
        "ep",
        split_axis=0,
        concat_axis=0,
        tiled=True,
    )
    slot_rows = received.reshape(slot_total, feature_count)
    gate_act = jnp.dot(slot_rows, gate_proj[0], preferred_element_type=jnp.float32)
    up_act = jnp.dot(slot_rows, up_proj[0], preferred_element_type=jnp.float32)
    hidden = (jax.nn.silu(gate_act) * up_act).astype(jnp.bfloat16)
    down_mat = down_proj[0]
    summed_t = lax.psum_scatter(
        lax.dot_general(
            down_mat, hidden, (((0,), (1,)), ((), ())), preferred_element_type=jnp.float32
        ).astype(jnp.bfloat16),
        "dp",
        scatter_dimension=0,
        tiled=True,
    ).astype(jnp.float32)
    summed = summed_t.T.astype(jnp.bfloat16).reshape(expert_count, capacity, column_count)
    returned = lax.all_to_all(summed, "ep", split_axis=0, concat_axis=0, tiled=True)
    weight_flat = all_weights.reshape(-1).astype(jnp.float32)
    weighted = jnp.sum(
        (placed * weight_flat[:, None]).reshape(token_total, top_count, slot_total), axis=1
    )
    mixed = jnp.dot(
        weighted,
        returned.reshape(slot_total, column_count).astype(jnp.float32),
        precision=lax.Precision.HIGHEST,
    ).astype(jnp.bfloat16)
    own = lax.all_to_all(
        mixed.reshape(group_count, token_count, column_count),
        "dp",
        split_axis=0,
        concat_axis=2,
        tiled=True,
    )
    return own.reshape(1, 1, token_count, feature_count)


def solution(mesh):
    placed = (
        P("ep", "dp", None, None),
        P("ep", "dp", None, None),
        P("ep", "dp", None, None),
        P("ep", None, "dp"),
        P("ep", None, "dp"),
        P("ep", "dp", None),
    )
    return jax.shard_map(
        body, mesh=mesh, in_specs=placed, out_specs=P("ep", "dp", None, None), check_vma=False
    )
```

profile of v0, /device:TPU:0, one launch (start us, length us, event | category | flops | bytes accessed | tf_op | source)
XLA Modules:
  0.0 90.4 jit_solution(14572636809706801968)
XLA Ops:
  6.5 0.0 reduce-scatter.2.cloned.1.call-start
  6.5 5.4 %all_gather.9 = s32[1,2,1,8]{3,2,0,1:T(1,128)S(1)} all-gather(s32[1,1,1,8]{3,2,0,1:T(1,128)} %bitcast.43), channel_id=1, replica_groups=mesh['dp'=2,'ep'=16] {'dp'}, dimensions={1}, use_global_device_ids=true | all-gather | bytes 96 | tf_op jit(solution)/shard_map/all_gather | solution.py:29
  11.9 0.5 broadcast.39
  12.4 0.7 fusion.32
  13.1 0.1 eq.30
  13.2 0.1 fusion.29
  13.3 0.2 select_reduce_fusion.1
  13.5 0.1 reduce_sum.30
  13.6 4.4 %all_gather.10 = bf16[1,2,1,8]{3,2,0,1:T(2,128)(2,1)S(1)} all-gather(bf16[1,1,1,8]{3,2,0,1:T(2,128)(2,1)} %bitcast.44), channel_id=1, replica_groups=mesh['dp'=2,'ep'=16] {'dp'}, dimensions={1}, use_global_device_ids=true | all-gather | bytes 48 | tf_op jit(solution)/shard_map/all_gather | solution.py:35
  17.9 4.6 %all_gather.11 = bf16[1,2,1,3584]{3,2,0,1:T(2,128)(2,1)S(1)} all-gather(bf16[1,1,1,3584]{3,2,0,1:T(2,128)(2,1)} %bitcast.40), channel_id=1, replica_groups=mesh['dp'=2,'ep'=16] {'dp'}, dimensions={1}, use_global_device_ids=true | all-gather | bytes 21504 | tf_op jit(solution)/shard_map/all_gather | solution.py:34
  22.6 0.1 convert_reduce_fusion
  22.6 0.3 convolution_convert_fusion
  22.9 0.1 reshape.70
  23.0 15.6 %all_to_all.19 = bf16[16,2,3584]{2,1,0:T(2,128)(2,1)S(1)} all-to-all(bf16[16,2,3584]{2,1,0:T(2,128)(2,1)S(1)} %reshape.70), channel_id=1, replica_groups=mesh['dp'=2,'ep'=16] {'ep'}, dimensions={0} | all-to-all | bytes 458752 | tf_op jit(solution)/shard_map/all_to_all | solution.py:42
  38.7 0.1 reshape.71
  38.7 4.4 %fusion.4 = f32[32,1024]{1,0:T(8,128)S(1)} fusion(bf16[32,3584]{1,0:T(8,128)(2,1)S(1)} %reshape.71, bf16[1,3584,1024]{2,1,0:T(8,128)(2,1)} %param.9), kind=kOutput, calls=%fused_computation.4 | convolution fusion | flops 234881024 | bytes 7700480 | tf_op jit(solution)/shard_map/dot_general | solution.py:50
  43.2 8.5 %fusion.9 = bf16[3584,32]{0,1:T(8,128)(2,1)} fusion(bf16[1,1024,3584]{2,1,0:T(8,128)(2,1)} %param.11, bf16[32,3584]{1,0:T(8,128)(2,1)S(1)} %reshape.71, bf16[1,3584,1024]{2,1,0:T(8,128)(2,1)} %param.10, f32[32,1024]{1,0:T(8,128)S(1)} %fusion.4), kind=kOutput, calls=%fused_computation.8 | convolution fusion | flops 470073344 | bytes 15269888 | tf_op jit(solution)/shard_map/dot_general | solution.py:55
  51.7 0.0 reduce-scatter.2.cloned.1.call-update
  51.7 9.6 %reduce-scatter.2.cloned.1.call-done = bf16[1792,32]{0,1:T(8,128)(2,1)} async-done(((bf16[3584,32]{0,1:T(8,128)(2,1)}), bf16[1792,32]{0,1:T(8,128)(2,1)}) %reduce-scatter.2.cloned.1.call-update) | async-done | bytes 114704 | tf_op jit(solution)/shard_map/reduce_scatter | solution.py:54
  61.3 0.9 %reshape.72 = bf16[16,2,1792]{2,1,0:T(2,128)(2,1)S(1)} reshape(bf16[32,1792]{1,0:T(8,128)(2,1)} %bitcast.39) | data formatting | bytes 229376 | tf_op jit(solution)/shard_map/reshape | solution.py:62
  62.3 13.0 %all_to_all.20 = bf16[16,2,1792]{2,1,0:T(2,128)(2,1)S(1)} all-to-all(bf16[16,2,1792]{2,1,0:T(2,128)(2,1)S(1)} %reshape.72), channel_id=1, replica_groups=mesh['dp'=2,'ep'=16] {'ep'}, dimensions={0} | all-to-all | bytes 229376 | tf_op jit(solution)/shard_map/all_to_all | solution.py:63
  75.4 0.2 fusion.12
  75.6 0.5 broadcast.40
  76.1 0.7 reduce.5
  76.8 6.1 %all_to_all.21 = bf16[2,2,896]{2,1,0:T(2,128)(2,1)S(1)} all-to-all(bf16[2,2,896]{2,1,0:T(2,128)(2,1)S(1)} %reshape.86), channel_id=1, replica_groups=mesh['dp'=2,'ep'=16] {'dp'}, dimensions={0} | all-to-all | bytes 14336 | tf_op jit(solution)/shard_map/all_to_all | solution.py:73
  82.9 0.6 reshape.87
  (5 shorter events, 0.1 us)
Async XLA Ops:
  6.5 54.8 %reduce-scatter.2.cloned.1.call-start = ((), (), s32[]{:S(2)}) async-start(), calls=%async_computation.4 | async-start | bytes 344064 | tf_op jit(solution)/shard_map/reduce_scatter | solution.py:54
Sparse Core Ops, SparseCore 0:
  51.8 9.4 reduce-scatter.1
where the time goes:
time: 90.7 us; the launch traced here: 90.4 us
  blocking collectives  49.2 us (54%)
  matrix products  13.4 us (15%)
  between operations  13.4 us (15%)
  waiting for transfers between devices  9.65 us (11%)
  local copies, waits for them, and re-layouts  3 us (3%)
  other arithmetic  1.72 us (2%)
    all_to_all x1, blocking collectives, body(): lax.all_to_all(buffer.reshape(expert_count, capacity, feature_count), 'ep...  15.6 us
    all_to_all x1, blocking collectives, body(): lax.all_to_all(summed, 'ep', split_axis=0, concat_axis=0, tiled=True)  13 us
    reduce_scatter x1, waiting for transfers between devices, body(): lax.psum_scatter(lax.dot_general(down_mat, hidden, (((0,), (1,)), ((), ()...  9.63 us
    dot_general x1, matrix products, body(): lax.dot_general(down_mat, hidden, (((0,), (1,)), ((), ())), preferred_ele...  8.5 us
    all_to_all x1, blocking collectives, body(): lax.all_to_all(mixed.reshape(group_count, token_count, column_count), 'dp...  6.14 us
    all_gather x1, blocking collectives, body(): all_ids = lax.all_gather(expert_ids, 'dp', axis=1, tiled=True)  5.38 us
    all_gather x1, blocking collectives, body(): lax.all_gather(tokens, 'dp', axis=1, tiled=True)  4.61 us
    dot_general x1, matrix products, body(): jnp.dot(slot_rows, gate_proj[0], preferred_element_type=jnp.float32)  4.45 us
  transfers between devices with their start and end apart: 1, of which 1 were waited for; matrix products, arithmetic and copies ran while one was open for 0% of the time, Pallas kernels for 0%

commit v1 on v0

--- a/solution.py
+++ b/solution.py
@@ -15,6 +15,13 @@
 
 
 def body(tokens, gate_weights, expert_ids, gate_proj, up_proj, down_proj):
+
+    def run_area(x_in, ax_name="dp"):
+        v_now = lax.all_to_all(
+            jnp.stack(jnp.split(x_in, lax.axis_size(ax_name), axis=0), axis=0), ax_name, 0, 0
+        )
+        return jnp.concatenate(v_now, axis=2)
+
     group_count = lax.axis_size("dp")
     expert_count = lax.axis_size("ep")
     token_count = tokens.shape[2]
@@ -70,13 +77,7 @@
         returned.reshape(slot_total, column_count).astype(jnp.float32),
         precision=lax.Precision.HIGHEST,
     ).astype(jnp.bfloat16)
-    own = lax.all_to_all(
-        mixed.reshape(group_count, token_count, column_count),
-        "dp",
-        split_axis=0,
-        concat_axis=2,
-        tiled=True,
-    )
+    own = run_area(mixed.reshape(group_count, token_count, column_count))
     return own.reshape(1, 1, token_count, feature_count)
 
 

time: 90.7 us -> 90.8 us (level)
  no operation moved by 1% of the time
where the time goes in v1:
time: 90.8 us; the launch traced here: 90.5 us
  blocking collectives  49.2 us (54%)
  matrix products  13.4 us (15%)
  between operations  13.4 us (15%)
  waiting for transfers between devices  9.65 us (11%)
  local copies, waits for them, and re-layouts  3.02 us (3%)
  other arithmetic  1.78 us (2%)
    all_to_all x1, blocking collectives, body(): lax.all_to_all(buffer.reshape(expert_count, capacity, feature_count), 'ep...  15.6 us
    all_to_all x1, blocking collectives, body(): lax.all_to_all(summed, 'ep', split_axis=0, concat_axis=0, tiled=True)  13 us
    reduce_scatter x1, waiting for transfers between devices, body(): lax.psum_scatter(lax.dot_general(down_mat, hidden, (((0,), (1,)), ((), ()...  9.63 us
    dot_general x1, matrix products, body(): lax.dot_general(down_mat, hidden, (((0,), (1,)), ((), ())), preferred_ele...  8.5 us
    all_to_all x1, blocking collectives, run_area(): lax.all_to_all(jnp.stack(jnp.split(x_in, lax.axis_size(ax_name), axis=0),...  6.14 us
    all_gather x1, blocking collectives, body(): all_ids = lax.all_gather(expert_ids, 'dp', axis=1, tiled=True)  5.38 us
    all_gather x1, blocking collectives, body(): lax.all_gather(tokens, 'dp', axis=1, tiled=True)  4.61 us
    dot_general x1, matrix products, body(): jnp.dot(slot_rows, gate_proj[0], preferred_element_type=jnp.float32)  4.45 us
  transfers between devices with their start and end apart: 1, of which 1 were waited for; matrix products, arithmetic and copies ran while one was open for 0% of the time, Pallas kernels for 0%

profile of v1, /device:TPU:0, one launch (start us, length us, event | category | flops | bytes accessed | tf_op | source)
XLA Modules:
  0.0 90.5 jit_solution(18156122526975307088)
XLA Ops:
  6.5 0.0 reduce-scatter.2.cloned.1.call-start
  6.5 5.4 %all_gather.9 = s32[1,2,1,8]{3,2,0,1:T(1,128)S(1)} all-gather(s32[1,1,1,8]{3,2,0,1:T(1,128)} %bitcast.45), channel_id=1, replica_groups=mesh['dp'=2,'ep'=16] {'dp'}, dimensions={1}, use_global_device_ids=true | all-gather | bytes 96 | tf_op jit(solution)/shard_map/all_gather | solution.py:36
  11.9 0.5 broadcast.39
  12.4 0.7 fusion.31
  13.1 0.1 eq.30
  13.2 0.1 fusion.28
  13.3 0.2 select_reduce_fusion.1
  13.5 0.1 reduce_sum.30
  13.6 4.4 %all_gather.10 = bf16[1,2,1,8]{3,2,0,1:T(2,128)(2,1)S(1)} all-gather(bf16[1,1,1,8]{3,2,0,1:T(2,128)(2,1)} %bitcast.46), channel_id=1, replica_groups=mesh['dp'=2,'ep'=16] {'dp'}, dimensions={1}, use_global_device_ids=true | all-gather | bytes 48 | tf_op jit(solution)/shard_map/all_gather | solution.py:42
  17.9 4.6 %all_gather.11 = bf16[1,2,1,3584]{3,2,0,1:T(2,128)(2,1)S(1)} all-gather(bf16[1,1,1,3584]{3,2,0,1:T(2,128)(2,1)} %bitcast.42), channel_id=1, replica_groups=mesh['dp'=2,'ep'=16] {'dp'}, dimensions={1}, use_global_device_ids=true | all-gather | bytes 21504 | tf_op jit(solution)/shard_map/all_gather | solution.py:41
  22.6 0.1 convert_reduce_fusion
  22.6 0.3 convolution_convert_fusion
  22.9 0.1 reshape.65
  23.0 15.6 %all_to_all.15 = bf16[16,2,3584]{2,1,0:T(2,128)(2,1)S(1)} all-to-all(bf16[16,2,3584]{2,1,0:T(2,128)(2,1)S(1)} %reshape.65), channel_id=1, replica_groups=mesh['dp'=2,'ep'=16] {'ep'}, dimensions={0} | all-to-all | bytes 458752 | tf_op jit(solution)/shard_map/all_to_all | solution.py:49
  38.7 0.1 reshape.66
  38.7 4.4 %fusion.4 = f32[32,1024]{1,0:T(8,128)S(1)} fusion(bf16[32,3584]{1,0:T(8,128)(2,1)S(1)} %reshape.66, bf16[1,3584,1024]{2,1,0:T(8,128)(2,1)} %param.9), kind=kOutput, calls=%fused_computation.4 | convolution fusion | flops 234881024 | bytes 7700480 | tf_op jit(solution)/shard_map/dot_general | solution.py:57
  43.2 8.5 %fusion.9 = bf16[3584,32]{0,1:T(8,128)(2,1)} fusion(bf16[1,1024,3584]{2,1,0:T(8,128)(2,1)} %param.11, bf16[32,3584]{1,0:T(8,128)(2,1)S(1)} %reshape.66, bf16[1,3584,1024]{2,1,0:T(8,128)(2,1)} %param.10, f32[32,1024]{1,0:T(8,128)S(1)} %fusion.4), kind=kOutput, calls=%fused_computation.8 | convolution fusion | flops 470073344 | bytes 15269888 | tf_op jit(solution)/shard_map/dot_general | solution.py:62
  51.7 0.0 reduce-scatter.2.cloned.1.call-update
  51.7 9.6 %reduce-scatter.2.cloned.1.call-done = bf16[1792,32]{0,1:T(8,128)(2,1)} async-done(((bf16[3584,32]{0,1:T(8,128)(2,1)}), bf16[1792,32]{0,1:T(8,128)(2,1)}) %reduce-scatter.2.cloned.1.call-update) | async-done | bytes 114704 | tf_op jit(solution)/shard_map/reduce_scatter | solution.py:61
  61.3 0.9 %reshape.67 = bf16[16,2,1792]{2,1,0:T(2,128)(2,1)S(1)} reshape(bf16[32,1792]{1,0:T(8,128)(2,1)} %bitcast.41) | data formatting | bytes 229376 | tf_op jit(solution)/shard_map/reshape | solution.py:69
  62.3 13.0 %all_to_all.16 = bf16[16,2,1792]{2,1,0:T(2,128)(2,1)S(1)} all-to-all(bf16[16,2,1792]{2,1,0:T(2,128)(2,1)S(1)} %reshape.67), channel_id=1, replica_groups=mesh['dp'=2,'ep'=16] {'ep'}, dimensions={0} | all-to-all | bytes 229376 | tf_op jit(solution)/shard_map/all_to_all | solution.py:70
  75.4 0.2 convolution_convert_fusion.1
  75.6 0.5 broadcast.40
  76.1 0.7 reduce.5
  76.8 6.1 %all_to_all.17 = bf16[2,2,896]{2,1,0:T(2,128)(2,1)S(1)} all-to-all(bf16[2,2,896]{2,1,0:T(2,128)(2,1)S(1)} %reshape.79), channel_id=1, replica_groups=mesh['dp'=2,'ep'=16] {'dp'}, dimensions={0} | all-to-all | bytes 14336 | tf_op jit(solution)/shard_map/all_to_all | solution.py:20
  83.0 0.6 reshape.80
  (7 shorter events, 0.2 us)
Async XLA Ops:
  6.5 54.8 %reduce-scatter.2.cloned.1.call-start = ((), (), s32[]{:S(2)}) async-start(), calls=%async_computation.4 | async-start | bytes 344064 | tf_op jit(solution)/shard_map/reduce_scatter | solution.py:61
Sparse Core Ops, SparseCore 0:
  51.8 9.4 reduce-scatter.1
